TPU v7x, 128 devices: a whole 4x4x4 slice. The times are simulated.
128 devices in a mesh: dp: 16 (over z, y), expert: 8 (over x, core).
Axes of the slice: x: 4, y: 4, z: 4, core: 2. Of those that a mesh axis runs over, the one named last changes fastest.
Arguments:
- tokens: bfloat16 [2048, 4096], P('dp'), may hold values from -6 to 6
- expert_ids: int32 [2048, 2], P('dp'), may hold values from 0 to 7, all different within a row; in each aligned block of 128 rows (0 to 127, 128 to 255, ...) at most 96 rows name the same one
- gate_weights: float32 [2048, 2], P('dp'), may hold values from 0.2 to 1
- live_counts: int32 [16], P('dp'), may hold values from 64 to 128, as said below
- w_gate: bfloat16 [8, 4096, 8192], P('expert', None, 'dp'), may hold values from -0.09375 to 0.09375
- w_up: bfloat16 [8, 4096, 8192], P('expert', None, 'dp'), may hold values from -0.09375 to 0.09375
- w_down: bfloat16 [8, 8192, 4096], P('expert', 'dp'), may hold values from -0.0625 to 0.0625
Outputs:
- mixed: bfloat16 [2048, 4096], P('dp')
- total_loads: int32 [8], replicated
Inputs may be any that keep to these rules, and one draw needn't show every extreme that they name: `expert_ids`: each token names two different experts. Among the tokens of one rank no expert is named more than 96 times, a bound that some block reaches in some ranks. Rank r's first live_counts[r] tokens are live, the rest are padding. Some rank has all 128 tokens live.
All inputs are finite; a program needn't handle non-finite values.
Results may differ from a plain program's by a relative error of at most 0.017.
Values may be sent and summed in bfloat16 or wider, within the bound.
No kernel may reach another device: no remote copies, remote signals or barrier semaphores. Data moves between devices by JAX's collectives and lax.ppermute only.
A program may use at most 128 MiB of HBM per device.

v0:
```python
import functools

import jax
import jax.numpy as jnp
from jax import lax
from jax.experimental import pallas as pl
from jax.experimental.pallas import tpu as pltpu
from jax.sharding import Mesh
from jax.sharding import PartitionSpec as P

DP = ("z", "y")
PLANE = ("z", "y", "c")
LANES = 128
STEP = 1024


def plane_perm(stage, shift, nz, ny):
    pairs = []
    for z in range(nz):
        for y in range(ny):
            for c in range(2):
                along_y = (stage == 1) == (c == 0)
                to_z, to_y = (z, (y + shift) % ny) if along_y else ((z + shift) % nz, y)
                pairs.append(((z * ny + y) * 2 + c, (to_z * ny + to_y) * 2 + c))
    return pairs


def hop(value, stage, shift):
    perm = plane_perm(stage, shift, lax.axis_size("z"), lax.axis_size("y"))
    return lax.ppermute(value, PLANE, perm)


def swap(value):
    return lax.ppermute(value, "c", [(0, 1), (1, 0)])


def total_of(*parts):
    return sum(part.astype(jnp.float32) for part in parts).astype(jnp.bfloat16)


def silu(v):
    return v / (1.0 + jnp.exp(-v))


def expert_kernel(n, width, my_expert, *refs):
    blocks, (gate, up, down), outs, loads = refs[:n], refs[n : n + 3], refs[n + 3 : 2 * n + 3], refs[2 * n + 3]
    hidden, weight = refs[2 * n + 4 :]
    mine = my_expert[0].astype(jnp.float32)
    counted = jnp.zeros((1, LANES), jnp.float32)
    rows = blocks[0].shape[0]
    for i, block in enumerate(blocks):
        x = block[:, :width]
        g = jnp.dot(x, gate[...], preferred_element_type=jnp.float32)
        u = jnp.dot(x, up[...], preferred_element_type=jnp.float32)
        hidden[i * rows : (i + 1) * rows] = (silu(g) * u).astype(jnp.bfloat16)
        route = block[:, width:].astype(jnp.float32)
        first, second = route[:, 0:1], route[:, 1:2]
        w_first = route[:, 2:3] + route[:, 3:4] + route[:, 4:5]
        w_second = route[:, 5:6] + route[:, 6:7] + route[:, 7:8]
        w = jnp.where(first == mine, w_first, 0.0) + jnp.where(second == mine, w_second, 0.0)
        weight[i * rows : (i + 1) * rows] = jnp.broadcast_to(w, (rows, LANES))
        lane = lax.broadcasted_iota(jnp.int32, route.shape, 1).astype(jnp.float32)
        named = (lane == first).astype(jnp.float32) + (lane == second).astype(jnp.float32)
        counted = counted + jnp.sum(named, axis=0, keepdims=True)
    loads[...] = jnp.broadcast_to(counted, loads.shape)

    def columns(k, _):
        at = pl.ds(pl.multiple_of(k * STEP, STEP), STEP)
        y = jnp.dot(hidden[...], down[:, at], preferred_element_type=jnp.float32)
        y = (y * weight[:, :1]).astype(jnp.bfloat16)
        for i, out in enumerate(outs):
            out[:, at] = y[i * rows : (i + 1) * rows]
        return 0

    lax.fori_loop(0, width // STEP, columns, 0)


def experts(blocks, my_expert, matrices):
    width, hidden = matrices[0].shape
    flops = 6 * sum(block.shape[0] for block in blocks) * width * hidden
    vmem = pl.BlockSpec(memory_space=pltpu.VMEM)
    blocks = [pltpu.with_memory_space_constraint(block, pltpu.VMEM) for block in blocks]
    *outs, loads = pl.pallas_call(
        functools.partial(expert_kernel, len(blocks), width),
        in_specs=[pl.BlockSpec(memory_space=pltpu.SMEM)] + [vmem] * (len(blocks) + 3),
        out_specs=[vmem] * (len(blocks) + 1),
        out_shape=[jax.ShapeDtypeStruct((block.shape[0], width), jnp.bfloat16) for block in blocks]
        + [jax.ShapeDtypeStruct((8, LANES), jnp.float32)],
        scratch_shapes=[
            pltpu.VMEM((sum(block.shape[0] for block in blocks), hidden), jnp.bfloat16),
            pltpu.VMEM((sum(block.shape[0] for block in blocks), LANES), jnp.float32),
        ],
        cost_estimate=pl.CostEstimate(flops=flops, bytes_accessed=1 << 24, transcendentals=0),
        compiler_params=pltpu.CompilerParams(vmem_limit_bytes=20 << 20),
        name="experts",
    )(my_expert, *blocks, *matrices)
    return outs, loads


def pack(tokens, expert_ids, gate_weights, live_counts, start):
    count, width = tokens.shape
    rows = count // 2

    def kernel(live, first, tokens, ids, gates, out):
        at = pl.ds(pl.multiple_of(first[0], rows), rows)
        out[:, :width] = tokens[at, :]
        place = lax.broadcasted_iota(jnp.int32, (2, count), 1)
        lines = [jnp.where(place < live[0], ids[...], -1).astype(jnp.float32)]
        rest, terms = gates[...], []
        for _ in range(3):
            terms.append(rest.astype(jnp.bfloat16).astype(jnp.float32))
            rest = rest - terms[-1]
        lines += [term[k : k + 1] for k in range(2) for term in terms]
        lines.append(jnp.zeros((LANES - 8, count), jnp.float32))
        columns = jnp.concatenate(lines, axis=0).T
        low, high = columns[:rows], columns[rows:]
        out[:, width:] = jnp.where(first[0] == 0, low, high).astype(jnp.bfloat16)

    smem, vmem = pl.BlockSpec(memory_space=pltpu.SMEM), pl.BlockSpec(memory_space=pltpu.VMEM)
    return pl.pallas_call(
        kernel,
        in_specs=[smem, smem, vmem, vmem, vmem],
        out_specs=vmem,
        out_shape=jax.ShapeDtypeStruct((rows, width + LANES), jnp.bfloat16),
        compiler_params=pltpu.CompilerParams(vmem_limit_bytes=8 << 20),
        name="pack",
    )(live_counts, start.astype(jnp.int32).reshape(1), tokens, expert_ids.T, gate_weights.T)


def staged(my_expert, matrices):
    def kernel(expert, gate, up, down, out):
        out[0] = expert[0]

    smem, vmem = pl.BlockSpec(memory_space=pltpu.SMEM), pl.BlockSpec(memory_space=pltpu.VMEM)
    return pl.pallas_call(
        kernel,
        in_specs=[smem, vmem, vmem, vmem],
        out_specs=smem,
        out_shape=jax.ShapeDtypeStruct((1,), jnp.int32),
        compiler_params=pltpu.CompilerParams(vmem_limit_bytes=1 << 20),
        name="stage",
    )(my_expert, *matrices)


def layer(tokens, expert_ids, gate_weights, live_counts, w_gate, w_up, w_down):
    core = lax.axis_index("c")
    x_at = lax.axis_index("x")
    n_x = lax.axis_size("x")
    my_expert = (x_at * 2 + core).astype(jnp.int32).reshape(1)
    n_experts = n_x * 2
    rows = tokens.shape[0] // 2
    start = core * rows

    matrices = tuple(pltpu.with_memory_space_constraint(m[0], pltpu.VMEM) for m in (w_gate, w_up, w_down))
    packed = pack(tokens, expert_ids, gate_weights, live_counts, start)
    loads = []

    my_expert = staged(my_expert, matrices)
    low = jnp.concatenate([packed, hop(packed, 1, -1)])
    high = jnp.concatenate([hop(packed, 1, 1), hop(packed, 1, 2)])
    behind_low = hop(low, 2, 1)
    ahead_high = hop(high, 2, -1)
    ahead_low = hop(low, 2, -1)
    behind_high = hop(high, 2, 1)
    far_low = hop(behind_low, 2, 1)
    far_high = hop(ahead_high, 2, -1)

    def run(*blocks):
        shared = [swap(block) for block in blocks]
        outs, counted = experts((*blocks, *shared), my_expert, matrices)
        loads.append(counted)
        mine, others = outs[: len(blocks)], outs[len(blocks) :]
        back = [swap(other) for other in others]
        return lax.optimization_barrier([total_of(*pair) for pair in zip(mine, back)])

    low, high = run(low, high)
    behind_low, ahead_high = run(behind_low, ahead_high)
    ahead_low, behind_high = run(ahead_low, behind_high)
    far_low, far_high = run(far_low, far_high)

    from_ahead_low = hop(behind_low, 2, -1)
    from_behind_high = hop(ahead_high, 2, 1)
    from_behind_low = hop(ahead_low, 2, 1)
    from_ahead_high = hop(behind_high, 2, -1)
    from_far_low = hop(far_low, 2, 2)
    from_far_high = hop(far_high, 2, 2)
    near = total_of(low, from_ahead_low, from_behind_low, from_far_low)
    further = total_of(high, from_ahead_high, from_behind_high, from_far_high)
    plane_sum = total_of(
        near[:rows],
        hop(near[rows:], 1, 1),
        hop(further[:rows], 1, -1),
        hop(further[rows:], 1, 2),
    )

    share_rows = rows // n_x
    shares = plane_sum.reshape(n_x, share_rows, -1)
    shares = lax.all_to_all(shares, "x", 0, 0, tiled=True)
    share = jnp.sum(shares.astype(jnp.float32), axis=0).astype(jnp.bfloat16)
    shares = lax.all_to_all(jnp.broadcast_to(share, shares.shape), "x", 0, 0, tiled=True)
    half_out = shares.reshape(rows, -1)
    other = swap(half_out)
    mixed = jnp.where(core == 0, jnp.concatenate([half_out, other]), jnp.concatenate([other, half_out]))
    total_loads = sum(loads)[0, :n_experts].astype(jnp.int32)
    return (mixed, total_loads)


def solution(mesh):
    torus = Mesh(mesh.devices.reshape(4, 4, mesh.shape["expert"] // 2, 2), ("z", "y", "x", "c"))
    expert = ("x", "c")
    in_specs = (
        P(DP, None),
        P(DP, None),
        P(DP, None),
        P(DP),
        P(expert, None, DP),
        P(expert, None, DP),
        P(expert, DP, None),
    )
    out_specs = (P(DP, None), P())
    return jax.shard_map(layer, mesh=torus, in_specs=in_specs, out_specs=out_specs, check_vma=False)
```

profile of v0, /device:TPU:2, one launch (start us, length us, event | category | flops | bytes accessed | tf_op | source)
XLA Modules:
  0.0 212.5 jit_solution(4737564267288255180)
XLA Ops:
  4.0 3.1 %collective-permute-start = (bf16[64,4224]{1,0:T(8,128)(2,1)S(1)}, bf16[64,4224]{1,0:T(8,128)(2,1)S(1)}, u32[]{:S(2)}, u32[]{:S(2)}) collective-permute-start(bf16[64,4224]{1,0:T(8,128)(2,1)S(1)} %pack.1), channel_id=1, source_target_pairs={{0,24},{1,97},{8,0},{9,105},{16,8},{17,113},{24,16},{25,121},{32,5... | collective-permute-start | bytes 1622024 | tf_op jit(solution)/shard_map/ppermute | solution.py:30
  7.1 2.2 %collective-permute-start.2 = (bf16[64,4224]{1,0:T(8,128)(2,1)S(1)}, bf16[64,4224]{1,0:T(8,128)(2,1)S(1)}, u32[]{:S(2)}, u32[]{:S(2)}) collective-permute-start(bf16[64,4224]{1,0:T(8,128)(2,1)S(1)} %pack.1), channel_id=1, source_target_pairs={{0,16},{1,65},{8,24},{9,73},{16,0},{17,81},{24,8},{25,89},{32,48},... | collective-permute-start | bytes 1622024 | tf_op jit(solution)/shard_map/ppermute | solution.py:30
  9.3 10.5 %collective-permute-done = bf16[64,4224]{1,0:T(8,128)(2,1)S(1)} collective-permute-done((bf16[64,4224]{1,0:T(8,128)(2,1)S(1)}, bf16[64,4224]{1,0:T(8,128)(2,1)S(1)}, u32[]{:S(2)}, u32[]{:S(2)}) %collective-permute-start) | collective-permute-done | bytes 540704 | tf_op jit(solution)/shard_map/ppermute | solution.py:30
  23.5 4.1 %collective-permute-start.8 = (bf16[128,4224]{1,0:T(8,128)(2,1)S(1)}, bf16[128,4224]{1,0:T(8,128)(2,1)}, u32[]{:S(2)}, u32[]{:S(2)}) collective-permute-start(bf16[128,4224]{1,0:T(8,128)(2,1)S(1)} %constant_dynamic-update-slice_fusion.refs_1_), channel_id=1, source_target_pairs={{0,96},{1,25},{8,104},{9,1},{16,112},{17,9},{24,120},{25,17},{32,0... | collective-permute-start | bytes 3244040 | tf_op jit(solution)/shard_map/ppermute | solution.py:30
  27.7 4.2 %collective-permute-start.14 = (bf16[128,4224]{1,0:T(8,128)(2,1)S(1)}, bf16[128,4224]{1,0:T(8,128)(2,1)S(1)}, u32[]{:S(2)}, u32[]{:S(2)}) collective-permute-start(bf16[128,4224]{1,0:T(8,128)(2,1)S(1)} %pad_maximum_fusion.refs_0_), channel_id=1, source_target_pairs={{0,96},{1,25},{8,104},{9,1},{16,112},{17,9},{24,120},{25,17},{32,0... | collective-permute-start | bytes 3244040 | tf_op jit(solution)/shard_map/ppermute | solution.py:30
  31.8 5.2 %collective-permute-done.7.refs_0_ = bf16[128,4224]{1,0:T(8,128)(2,1)S(1)} collective-permute-done((bf16[128,4224]{1,0:T(8,128)(2,1)S(1)}, bf16[128,4224]{1,0:T(8,128)(2,1)S(1)}, u32[]{:S(2)}, u32[]{:S(2)}) %collective-permute-start.7) | collective-permute-done | bytes 1081376 | tf_op jit(solution)/shard_map/ppermute | solution.py:30
  37.0 5.4 %collective-permute-done.8.refs_1_ = bf16[128,4224]{1,0:T(8,128)(2,1)} collective-permute-done((bf16[128,4224]{1,0:T(8,128)(2,1)S(1)}, bf16[128,4224]{1,0:T(8,128)(2,1)}, u32[]{:S(2)}, u32[]{:S(2)}) %collective-permute-start.8) | collective-permute-done | bytes 1081376 | tf_op jit(solution)/shard_map/ppermute | solution.py:30
  42.9 11.0 %collective-permute-done.14.refs_0_ = bf16[128,4224]{1,0:T(8,128)(2,1)S(1)} collective-permute-done((bf16[128,4224]{1,0:T(8,128)(2,1)S(1)}, bf16[128,4224]{1,0:T(8,128)(2,1)S(1)}, u32[]{:S(2)}, u32[]{:S(2)}) %collective-permute-start.14) | collective-permute-done | bytes 1081376 | tf_op jit(solution)/shard_map/ppermute | solution.py:30
  54.9 2.2 %copy-done = bf16[1,4096,512]{2,1,0:T(8,128)(2,1)S(1)} copy-done((bf16[1,4096,512]{2,1,0:T(8,128)(2,1)S(1)}, bf16[1,4096,512]{2,1,0:T(8,128)(2,1)}, u32[]{:S(2)}) %copy-start) | copy-done | bytes 4194328
  57.1 2.2 %copy-done.2 = bf16[1,4096,512]{2,1,0:T(8,128)(2,1)S(1)} copy-done((bf16[1,4096,512]{2,1,0:T(8,128)(2,1)S(1)}, bf16[1,4096,512]{2,1,0:T(8,128)(2,1)}, u32[]{:S(2)}) %copy-start.2) | copy-done | bytes 4194328
  66.1 10.2 %experts.5 = (bf16[128,4096]{1,0:T(8,128)(2,1)S(1)}, bf16[128,4096]{1,0:T(8,128)(2,1)S(1)}, bf16[128,4096]{1,0:T(8,128)(2,1)S(1)}, bf16[128,4096]{1,0:T(8,128)(2,1)S(1)}, f32[8,128]{1,0:T(8,128)S(1)}) custom-call(s32[1]{0:T(128)} %stage.1.my_expert, bf16[128,4224]{1,0:T(8,128)(2,1)S(1)} %collective-permute-done.7.refs_0_, ...), custom_call_target="tpu_custom_call" | custom-call | flops 6442450944 | bytes 16777216 | tf_op jit(solution)/shard_map/experts/pallas_call | solution.py:83
  76.3 2.3 %collective-permute-start.22 = (bf16[128,4224]{1,0:T(8,128)(2,1)}, bf16[128,4224]{1,0:T(8,128)(2,1)S(1)}, u32[]{:S(2)}, u32[]{:S(2)}) collective-permute-start(bf16[128,4224]{1,0:T(8,128)(2,1)} %collective-permute-done.8.refs_1_), channel_id=1, source_target_pairs={{0,96},{1,25},{8,104},{9,1},{16,112},{17,9},{24,120},{25,17},{32,0... | collective-permute-start | bytes 3244040 | tf_op jit(solution)/shard_map/ppermute | solution.py:30
  78.6 9.9 %experts.4 = (bf16[128,4096]{1,0:T(8,128)(2,1)S(1)}, bf16[128,4096]{1,0:T(8,128)(2,1)S(1)}, bf16[128,4096]{1,0:T(8,128)(2,1)S(1)}, bf16[128,4096]{1,0:T(8,128)(2,1)S(1)}, f32[8,128]{1,0:T(8,128)S(1)}) custom-call(s32[1]{0:T(128)} %stage.1.my_expert, bf16[128,4224]{1,0:T(8,128)(2,1)S(1)} %pad_maximum_fusion.refs_0_, ...), custom_call_target="tpu_custom_call" | custom-call | flops 6442450944 | bytes 16777216 | tf_op jit(solution)/shard_map/experts/pallas_call | solution.py:83
  89.1 9.6 %experts.6 = (bf16[128,4096]{1,0:T(8,128)(2,1)S(1)}, bf16[128,4096]{1,0:T(8,128)(2,1)S(1)}, bf16[128,4096]{1,0:T(8,128)(2,1)S(1)}, bf16[128,4096]{1,0:T(8,128)(2,1)S(1)}, f32[8,128]{1,0:T(8,128)S(1)}) custom-call(s32[1]{0:T(128)} %stage.1.my_expert, bf16[128,4224]{1,0:T(8,128)(2,1)S(1)} %copy-done.10, bf16[128,4224]{1,0:T(8,128)(2,1)} %collective-permute-done.15.refs_1_, ...), custom_call_target="tpu_custom_call" | custom-call | flops 6442450944 | bytes 16777216 | tf_op jit(solution)/shard_map/experts/pallas_call | solution.py:83
  100.5 2.6 %collective-permute-done.23.refs_2_ = bf16[128,4224]{1,0:T(8,128)(2,1)S(1)} collective-permute-done((bf16[128,4224]{1,0:T(8,128)(2,1)S(1)}, bf16[128,4224]{1,0:T(8,128)(2,1)S(1)}, u32[]{:S(2)}, u32[]{:S(2)}) %collective-permute-start.23) | collective-permute-done | bytes 1081376 | tf_op jit(solution)/shard_map/ppermute | solution.py:34
  105.1 8.2 %experts.7 = (bf16[128,4096]{1,0:T(8,128)(2,1)S(1)}, bf16[128,4096]{1,0:T(8,128)(2,1)S(1)}, bf16[128,4096]{1,0:T(8,128)(2,1)S(1)}, bf16[128,4096]{1,0:T(8,128)(2,1)S(1)}, f32[8,128]{1,0:T(8,128)S(1)}) custom-call(s32[1]{0:T(128)} %stage.1.my_expert, bf16[128,4224]{1,0:T(8,128)(2,1)S(1)} %collective-permute-done.21.refs_0_, ...), custom_call_target="tpu_custom_call" | custom-call | flops 6442450944 | bytes 16777216 | tf_op jit(solution)/shard_map/experts/pallas_call | solution.py:83
  116.1 2.7 %collective-permute-start.29 = (bf16[128,4096]{1,0:T(8,128)(2,1)S(1)}, bf16[128,4096]{1,0:T(8,128)(2,1)S(1)}, u32[]{:S(2)}, u32[]{:S(2)}) collective-permute-start(bf16[128,4096]{1,0:T(8,128)(2,1)S(1)} %add_convert_fusion.4), channel_id=1, source_target_pairs={{0,96},{1,25},{8,104},{9,1},{16,112},{17,9},{24,120},{25,17},{32,0... | collective-permute-start | bytes 3145736 | tf_op jit(solution)/shard_map/ppermute | solution.py:30
  122.1 3.0 %collective-permute-start.13 = (bf16[128,4096]{1,0:T(8,128)(2,1)S(1)}, bf16[128,4096]{1,0:T(8,128)(2,1)S(1)}, u32[]{:S(2)}, u32[]{:S(2)}) collective-permute-start(bf16[128,4096]{1,0:T(8,128)(2,1)S(1)} %add_convert_fusion.7), channel_id=1, source_target_pairs={{0,96},{1,25},{8,104},{9,1},{16,112},{17,9},{24,120},{25,17},{32,0... | collective-permute-start | bytes 3145736 | tf_op jit(solution)/shard_map/ppermute | solution.py:30
  125.5 16.8 %collective-permute-done.29 = bf16[128,4096]{1,0:T(8,128)(2,1)S(1)} collective-permute-done((bf16[128,4096]{1,0:T(8,128)(2,1)S(1)}, bf16[128,4096]{1,0:T(8,128)(2,1)S(1)}, u32[]{:S(2)}, u32[]{:S(2)}) %collective-permute-start.29) | collective-permute-done | bytes 1048608 | tf_op jit(solution)/shard_map/ppermute | solution.py:30
  143.1 8.7 %collective-permute-start.33 = (bf16[64,4096]{1,0:T(8,128)(2,1)S(1)}, bf16[64,4096]{1,0:T(8,128)(2,1)S(1)}, u32[]{:S(2)}, u32[]{:S(2)}) collective-permute-start(bf16[64,4096]{1,0:T(8,128)(2,1)S(1)} %get-tuple-element.59), channel_id=1, source_target_pairs={{0,16},{1,65},{8,24},{9,73},{16,0},{17,81},{24,8},{25,89},{32,48},... | collective-permute-start | bytes 1572872 | tf_op jit(solution)/shard_map/ppermute | solution.py:30
  151.8 24.3 %collective-permute-done.13 = bf16[128,4096]{1,0:T(8,128)(2,1)S(1)} collective-permute-done((bf16[128,4096]{1,0:T(8,128)(2,1)S(1)}, bf16[128,4096]{1,0:T(8,128)(2,1)S(1)}, u32[]{:S(2)}, u32[]{:S(2)}) %collective-permute-start.13) | collective-permute-done | bytes 1048608 | tf_op jit(solution)/shard_map/ppermute | solution.py:30
  177.7 9.5 %collective-permute-done.28 = bf16[64,4096]{1,0:T(8,128)(2,1)S(1)} collective-permute-done((bf16[64,4096]{1,0:T(8,128)(2,1)S(1)}, bf16[64,4096]{1,0:T(8,128)(2,1)S(1)}, u32[]{:S(2)}, u32[]{:S(2)}) %collective-permute-start.28) | collective-permute-done | bytes 524320 | tf_op jit(solution)/shard_map/ppermute | solution.py:30
  187.5 11.2 %all_to_all.10 = bf16[4,16,4096]{2,1,0:T(8,128)(2,1)S(1)} all-to-all(bf16[4,16,4096]{2,1,0:T(8,128)(2,1)S(1)} %bitcast.30), channel_id=1, replica_groups=mesh['z'=4,'y'=4,'x'=4,'c'=2] {'x'}, dimensions={0} | all-to-all | bytes 1048576 | tf_op jit(solution)/shard_map/all_to_all | solution.py:198
  198.9 10.5 %all_to_all.11 = bf16[4,16,4096]{2,1,0:T(8,128)(2,1)S(1)} all-to-all(bf16[4,16,4096]{2,1,0:T(8,128)(2,1)S(1)} %broadcast_in_dim.3), channel_id=1, replica_groups=mesh['z'=4,'y'=4,'x'=4,'c'=2] {'x'}, dimensions={0} | all-to-all | bytes 1048576 | tf_op jit(solution)/shard_map/all_to_all | solution.py:200
  (97 shorter events, 31.4 us)
Async XLA Ops:
  7.1 16.4 %collective-permute-start.2 = (bf16[64,4224]{1,0:T(8,128)(2,1)S(1)}, bf16[64,4224]{1,0:T(8,128)(2,1)S(1)}, u32[]{:S(2)}, u32[]{:S(2)}) collective-permute-start(bf16[64,4224]{1,0:T(8,128)(2,1)S(1)} %pack.1), channel_id=1, source_target_pairs={{0,16},{1,65},{8,24},{9,73},{16,0},{17,81},{24,8},{25,89},{32,48},... | collective-permute-start | bytes 1622024 | tf_op jit(solution)/shard_map/ppermute | solution.py:30
  19.8 17.2 %collective-permute-start.7 = (bf16[128,4224]{1,0:T(8,128)(2,1)S(1)}, bf16[128,4224]{1,0:T(8,128)(2,1)S(1)}, u32[]{:S(2)}, u32[]{:S(2)}) collective-permute-start(bf16[128,4224]{1,0:T(8,128)(2,1)S(1)} %pad_maximum_fusion.refs_0_), channel_id=1, source_target_pairs={{0,32},{1,9},{8,40},{9,17},{16,48},{17,25},{24,56},{25,1},{32,64},... | collective-permute-start | bytes 3244040 | tf_op jit(solution)/shard_map/ppermute | solution.py:30
  23.5 18.9 %collective-permute-start.8 = (bf16[128,4224]{1,0:T(8,128)(2,1)S(1)}, bf16[128,4224]{1,0:T(8,128)(2,1)}, u32[]{:S(2)}, u32[]{:S(2)}) collective-permute-start(bf16[128,4224]{1,0:T(8,128)(2,1)S(1)} %constant_dynamic-update-slice_fusion.refs_1_), channel_id=1, source_target_pairs={{0,96},{1,25},{8,104},{9,1},{16,112},{17,9},{24,120},{25,17},{32,0... | collective-permute-start | bytes 3244040 | tf_op jit(solution)/shard_map/ppermute | solution.py:30
  27.7 26.2 %collective-permute-start.14 = (bf16[128,4224]{1,0:T(8,128)(2,1)S(1)}, bf16[128,4224]{1,0:T(8,128)(2,1)S(1)}, u32[]{:S(2)}, u32[]{:S(2)}) collective-permute-start(bf16[128,4224]{1,0:T(8,128)(2,1)S(1)} %pad_maximum_fusion.refs_0_), channel_id=1, source_target_pairs={{0,96},{1,25},{8,104},{9,1},{16,112},{17,9},{24,120},{25,17},{32,0... | collective-permute-start | bytes 3244040 | tf_op jit(solution)/shard_map/ppermute | solution.py:30
  31.8 30.1 %collective-permute-start.15 = (bf16[128,4224]{1,0:T(8,128)(2,1)S(1)}, bf16[128,4224]{1,0:T(8,128)(2,1)}, u32[]{:S(2)}, u32[]{:S(2)}) collective-permute-start(bf16[128,4224]{1,0:T(8,128)(2,1)S(1)} %constant_dynamic-update-slice_fusion.refs_1_), channel_id=1, source_target_pairs={{0,32},{1,9},{8,40},{9,17},{16,48},{17,25},{24,56},{25,1},{32,64},... | collective-permute-start | bytes 3244040 | tf_op jit(solution)/shard_map/ppermute | solution.py:30
  37.0 27.0 %collective-permute-start.9 = (bf16[128,4224]{1,0:T(8,128)(2,1)S(1)}, bf16[128,4224]{1,0:T(8,128)(2,1)}, u32[]{:S(2)}, u32[]{:S(2)}) collective-permute-start(bf16[128,4224]{1,0:T(8,128)(2,1)S(1)} %collective-permute-done.7.refs_0_), channel_id=1, source_target_pairs={{0,1},{1,0},{2,3},{3,2},{4,5},{5,4},{6,7},{7,6},{8,9},{9,8},{10,11... | collective-permute-start | bytes 3244040 | tf_op jit(solution)/shard_map/ppermute | solution.py:34
  42.4 21.7 %collective-permute-start.10 = (bf16[128,4224]{1,0:T(8,128)(2,1)}, bf16[128,4224]{1,0:T(8,128)(2,1)}, u32[]{:S(2)}, u32[]{:S(2)}) collective-permute-start(bf16[128,4224]{1,0:T(8,128)(2,1)} %collective-permute-done.8.refs_1_), channel_id=1, source_target_pairs={{0,1},{1,0},{2,3},{3,2},{4,5},{5,4},{6,7},{7,6},{8,9},{9,8},{10,11... | collective-permute-start | bytes 3244040 | tf_op jit(solution)/shard_map/ppermute | solution.py:34
  42.4 33.9 %collective-permute-start.3 = (bf16[128,4224]{1,0:T(8,128)(2,1)S(1)}, bf16[128,4224]{1,0:T(8,128)(2,1)}, u32[]{:S(2)}, u32[]{:S(2)}) collective-permute-start(bf16[128,4224]{1,0:T(8,128)(2,1)S(1)} %pad_maximum_fusion.refs_0_), channel_id=1, source_target_pairs={{0,1},{1,0},{2,3},{3,2},{4,5},{5,4},{6,7},{7,6},{8,9},{9,8},{10,11... | collective-permute-start | bytes 3244040 | tf_op jit(solution)/shard_map/ppermute | solution.py:34
  54.9 23.7 %collective-permute-start.4 = (bf16[128,4224]{1,0:T(8,128)(2,1)S(1)}, bf16[128,4224]{1,0:T(8,128)(2,1)}, u32[]{:S(2)}, u32[]{:S(2)}) collective-permute-start(bf16[128,4224]{1,0:T(8,128)(2,1)S(1)} %constant_dynamic-update-slice_fusion.refs_1_), channel_id=1, source_target_pairs={{0,1},{1,0},{2,3},{3,2},{4,5},{5,4},{6,7},{7,6},{8,9},{9,8},{10,11... | collective-permute-start | bytes 3244040 | tf_op jit(solution)/shard_map/ppermute | solution.py:34
  62.0 36.8 %collective-permute-start.21 = (bf16[128,4224]{1,0:T(8,128)(2,1)S(1)}, bf16[128,4224]{1,0:T(8,128)(2,1)S(1)}, u32[]{:S(2)}, u32[]{:S(2)}) collective-permute-start(bf16[128,4224]{1,0:T(8,128)(2,1)S(1)} %collective-permute-done.7.refs_0_), channel_id=1, source_target_pairs={{0,32},{1,9},{8,40},{9,17},{16,48},{17,25},{24,56},{25,1},{32,64},... | collective-permute-start | bytes 3244040 | tf_op jit(solution)/shard_map/ppermute | solution.py:30
  64.1 24.4 %collective-permute-start.16 = (bf16[128,4224]{1,0:T(8,128)(2,1)}, bf16[128,4224]{1,0:T(8,128)(2,1)S(1)}, u32[]{:S(2)}, u32[]{:S(2)}) collective-permute-start(bf16[128,4224]{1,0:T(8,128)(2,1)} %copy-done.9), channel_id=1, source_target_pairs={{0,1},{1,0},{2,3},{3,2},{4,5},{5,4},{6,7},{7,6},{8,9},{9,8},{10,11... | collective-permute-start | bytes 3244040 | tf_op jit(solution)/shard_map/ppermute | solution.py:34
  64.1 24.9 %collective-permute-start.17 = (bf16[128,4224]{1,0:T(8,128)(2,1)}, bf16[128,4224]{1,0:T(8,128)(2,1)S(1)}, u32[]{:S(2)}, u32[]{:S(2)}) collective-permute-start(bf16[128,4224]{1,0:T(8,128)(2,1)} %collective-permute-done.15.refs_1_), channel_id=1, source_target_pairs={{0,1},{1,0},{2,3},{3,2},{4,5},{5,4},{6,7},{7,6},{8,9},{9,8},{10,11... | collective-permute-start | bytes 3244040 | tf_op jit(solution)/shard_map/ppermute | solution.py:34
  76.3 22.9 %collective-permute-start.22 = (bf16[128,4224]{1,0:T(8,128)(2,1)}, bf16[128,4224]{1,0:T(8,128)(2,1)S(1)}, u32[]{:S(2)}, u32[]{:S(2)}) collective-permute-start(bf16[128,4224]{1,0:T(8,128)(2,1)} %collective-permute-done.8.refs_1_), channel_id=1, source_target_pairs={{0,96},{1,25},{8,104},{9,1},{16,112},{17,9},{24,120},{25,17},{32,0... | collective-permute-start | bytes 3244040 | tf_op jit(solution)/shard_map/ppermute | solution.py:30
  78.6 20.8 %collective-permute-start.11 = (bf16[128,4096]{1,0:T(8,128)(2,1)S(1)}, bf16[128,4096]{1,0:T(8,128)(2,1)S(1)}, u32[]{:S(2)}, u32[]{:S(2)}) collective-permute-start(bf16[128,4096]{1,0:T(8,128)(2,1)S(1)} %get-tuple-element.36), channel_id=1, source_target_pairs={{0,1},{1,0},{2,3},{3,2},{4,5},{5,4},{6,7},{7,6},{8,9},{9,8},{10,11... | collective-permute-start | bytes 3145736 | tf_op jit(solution)/shard_map/ppermute | solution.py:34
  88.5 32.8 %collective-permute-start.5 = (bf16[128,4096]{1,0:T(8,128)(2,1)S(1)}, bf16[128,4096]{1,0:T(8,128)(2,1)S(1)}, u32[]{:S(2)}, u32[]{:S(2)}) collective-permute-start(bf16[128,4096]{1,0:T(8,128)(2,1)S(1)} %get-tuple-element.31), channel_id=1, source_target_pairs={{0,1},{1,0},{2,3},{3,2},{4,5},{5,4},{6,7},{7,6},{8,9},{9,8},{10,11... | collective-permute-start | bytes 3145736 | tf_op jit(solution)/shard_map/ppermute | solution.py:34
  98.7 22.9 %collective-permute-start.6 = (bf16[128,4096]{1,0:T(8,128)(2,1)S(1)}, bf16[128,4096]{1,0:T(8,128)(2,1)S(1)}, u32[]{:S(2)}, u32[]{:S(2)}) collective-permute-start(bf16[128,4096]{1,0:T(8,128)(2,1)S(1)} %get-tuple-element.33), channel_id=1, source_target_pairs={{0,1},{1,0},{2,3},{3,2},{4,5},{5,4},{6,7},{7,6},{8,9},{9,8},{10,11... | collective-permute-start | bytes 3145736 | tf_op jit(solution)/shard_map/ppermute | solution.py:34
  104.6 20.6 %collective-permute-start.30 = (bf16[128,4096]{1,0:T(8,128)(2,1)S(1)}, bf16[128,4096]{1,0:T(8,128)(2,1)S(1)}, u32[]{:S(2)}, u32[]{:S(2)}) collective-permute-start(bf16[128,4096]{1,0:T(8,128)(2,1)S(1)} %add_convert_fusion.6), channel_id=1, source_target_pairs={{0,32},{1,9},{8,40},{9,17},{16,48},{17,25},{24,56},{25,1},{32,64},... | collective-permute-start | bytes 3145736 | tf_op jit(solution)/shard_map/ppermute | solution.py:30
  116.1 26.3 %collective-permute-start.29 = (bf16[128,4096]{1,0:T(8,128)(2,1)S(1)}, bf16[128,4096]{1,0:T(8,128)(2,1)S(1)}, u32[]{:S(2)}, u32[]{:S(2)}) collective-permute-start(bf16[128,4096]{1,0:T(8,128)(2,1)S(1)} %add_convert_fusion.4), channel_id=1, source_target_pairs={{0,96},{1,25},{8,104},{9,1},{16,112},{17,9},{24,120},{25,17},{32,0... | collective-permute-start | bytes 3145736 | tf_op jit(solution)/shard_map/ppermute | solution.py:30
  119.3 23.1 %collective-permute-start.31 = (bf16[128,4096]{1,0:T(8,128)(2,1)S(1)}, bf16[128,4096]{1,0:T(8,128)(2,1)S(1)}, u32[]{:S(2)}, u32[]{:S(2)}) collective-permute-start(bf16[128,4096]{1,0:T(8,128)(2,1)S(1)} %add_convert_fusion.2), channel_id=1, source_target_pairs={{0,64},{1,17},{8,72},{9,25},{16,80},{17,1},{24,88},{25,9},{32,96},... | collective-permute-start | bytes 3145736 | tf_op jit(solution)/shard_map/ppermute | solution.py:30
  121.9 29.9 %collective-permute-start.20 = (bf16[128,4096]{1,0:T(8,128)(2,1)S(1)}, bf16[128,4096]{1,0:T(8,128)(2,1)S(1)}, u32[]{:S(2)}, u32[]{:S(2)}) collective-permute-start(bf16[128,4096]{1,0:T(8,128)(2,1)S(1)} %add_convert_fusion.5), channel_id=1, source_target_pairs={{0,32},{1,9},{8,40},{9,17},{16,48},{17,25},{24,56},{25,1},{32,64},... | collective-permute-start | bytes 3145736 | tf_op jit(solution)/shard_map/ppermute | solution.py:30
  122.1 53.9 %collective-permute-start.13 = (bf16[128,4096]{1,0:T(8,128)(2,1)S(1)}, bf16[128,4096]{1,0:T(8,128)(2,1)S(1)}, u32[]{:S(2)}, u32[]{:S(2)}) collective-permute-start(bf16[128,4096]{1,0:T(8,128)(2,1)S(1)} %add_convert_fusion.7), channel_id=1, source_target_pairs={{0,96},{1,25},{8,104},{9,1},{16,112},{17,9},{24,120},{25,17},{32,0... | collective-permute-start | bytes 3145736 | tf_op jit(solution)/shard_map/ppermute | solution.py:30
  125.2 50.9 %collective-permute-start.27 = (bf16[128,4096]{1,0:T(8,128)(2,1)S(1)}, bf16[128,4096]{1,0:T(8,128)(2,1)S(1)}, u32[]{:S(2)}, u32[]{:S(2)}) collective-permute-start(bf16[128,4096]{1,0:T(8,128)(2,1)S(1)} %add_convert_fusion.3), channel_id=1, source_target_pairs={{0,64},{1,17},{8,72},{9,25},{16,80},{17,1},{24,88},{25,9},{32,96},... | collective-permute-start | bytes 3145736 | tf_op jit(solution)/shard_map/ppermute | solution.py:30
  143.1 34.6 %collective-permute-start.33 = (bf16[64,4096]{1,0:T(8,128)(2,1)S(1)}, bf16[64,4096]{1,0:T(8,128)(2,1)S(1)}, u32[]{:S(2)}, u32[]{:S(2)}) collective-permute-start(bf16[64,4096]{1,0:T(8,128)(2,1)S(1)} %get-tuple-element.59), channel_id=1, source_target_pairs={{0,16},{1,65},{8,24},{9,73},{16,0},{17,81},{24,8},{25,89},{32,48},... | collective-permute-start | bytes 1572872 | tf_op jit(solution)/shard_map/ppermute | solution.py:30
  151.8 26.0 %collective-permute-start.32 = (bf16[64,4096]{1,0:T(8,128)(2,1)S(1)}, bf16[64,4096]{1,0:T(8,128)(2,1)S(1)}, u32[]{:S(2)}, u32[]{:S(2)}) collective-permute-start(bf16[64,4096]{1,0:T(8,128)(2,1)S(1)} %get-tuple-element.58), channel_id=1, source_target_pairs={{0,24},{1,97},{8,0},{9,105},{16,8},{17,113},{24,16},{25,121},{32,5... | collective-permute-start | bytes 1572872 | tf_op jit(solution)/shard_map/ppermute | solution.py:30
  (22 other events, 128.6 us)
where the time goes:
time: 215 us; the launch traced here: 212 us
  waiting for transfers between devices  91 us (42%)
  starting transfers between devices  42.4 us (20%)
  Pallas kernels  38.5 us (18%)
  blocking collectives  21.7 us (10%)
  local copies, waits for them, and re-layouts  11.8 us (5%)
  other arithmetic  5.45 us (3%)
    ppermute x18, waiting for transfers between devices, hop(): return lax.ppermute(value, PLANE, perm)  84.3 us
    ppermute x18, starting transfers between devices, hop(): return lax.ppermute(value, PLANE, perm)  38.5 us
    pallas_call x4, Pallas kernels, experts(): pl.pallas_call(functools.partial(expert_kernel, len(blocks), width), in_s...  37.9 us
    unnamed x23, local copies, waits for them, and re-layouts  11.6 us
    all_to_all x1, blocking collectives, layer(): shares = lax.all_to_all(shares, 'x', 0, 0, tiled=True)  11.2 us
    all_to_all x1, blocking collectives, layer(): lax.all_to_all(jnp.broadcast_to(share, shares.shape), 'x', 0, 0, tiled=True)  10.5 us
    ppermute x17, waiting for transfers between devices, swap(): return lax.ppermute(value, 'c', [(0, 1), (1, 0)])  6.7 us
  transfers between devices with their start and end apart: 35, of which 12 were waited for; matrix products, arithmetic and copies ran while one was open for 2% of the time, Pallas kernels for 18%

commit v1 on v0

--- a/solution.py
+++ b/solution.py
@@ -34,6 +34,11 @@
     return lax.ppermute(value, "c", [(0, 1), (1, 0)])
 
 
+def x_hop(value, shift):
+    size = lax.axis_size("x")
+    return lax.ppermute(value, "x", [(i, (i + shift) % size) for i in range(size)])
+
+
 def total_of(*parts):
     return sum(part.astype(jnp.float32) for part in parts).astype(jnp.bfloat16)
 
@@ -42,54 +47,60 @@
     return v / (1.0 + jnp.exp(-v))
 
 
-def expert_kernel(n, width, my_expert, *refs):
+def expert_kernel(n, width, rolled, my_expert, *refs):
     blocks, (gate, up, down), outs, loads = refs[:n], refs[n : n + 3], refs[n + 3 : 2 * n + 3], refs[2 * n + 3]
-    hidden, weight = refs[2 * n + 4 :]
+    hidden = refs[2 * n + 4]
+    units = hidden.shape[1]
+
+    def expand(at):
+        x = jnp.concatenate([block[:, :width] for block in blocks])
+        g = jnp.dot(x, gate[:, at], preferred_element_type=jnp.float32)
+        u = jnp.dot(x, up[:, at], preferred_element_type=jnp.float32)
+        return (silu(g) * u).astype(jnp.bfloat16)
+
+    if rolled:
+        part = units // 2
+
+        def step(k, _):
+            at = pl.ds(pl.multiple_of(k * part, part), part)
+            hidden[:, at] = expand(at)
+            return 0
+
+        lax.fori_loop(0, 2, step, 0)
+        held = hidden[...]
+    else:
+        held = expand(slice(0, units))
+
     mine = my_expert[0].astype(jnp.float32)
-    counted = jnp.zeros((1, LANES), jnp.float32)
-    rows = blocks[0].shape[0]
-    for i, block in enumerate(blocks):
-        x = block[:, :width]
-        g = jnp.dot(x, gate[...], preferred_element_type=jnp.float32)
-        u = jnp.dot(x, up[...], preferred_element_type=jnp.float32)
-        hidden[i * rows : (i + 1) * rows] = (silu(g) * u).astype(jnp.bfloat16)
-        route = block[:, width:].astype(jnp.float32)
-        first, second = route[:, 0:1], route[:, 1:2]
-        w_first = route[:, 2:3] + route[:, 3:4] + route[:, 4:5]
-        w_second = route[:, 5:6] + route[:, 6:7] + route[:, 7:8]
-        w = jnp.where(first == mine, w_first, 0.0) + jnp.where(second == mine, w_second, 0.0)
-        weight[i * rows : (i + 1) * rows] = jnp.broadcast_to(w, (rows, LANES))
-        lane = lax.broadcasted_iota(jnp.int32, route.shape, 1).astype(jnp.float32)
-        named = (lane == first).astype(jnp.float32) + (lane == second).astype(jnp.float32)
-        counted = counted + jnp.sum(named, axis=0, keepdims=True)
-    loads[...] = jnp.broadcast_to(counted, loads.shape)
-
-    def columns(k, _):
-        at = pl.ds(pl.multiple_of(k * STEP, STEP), STEP)
-        y = jnp.dot(hidden[...], down[:, at], preferred_element_type=jnp.float32)
-        y = (y * weight[:, :1]).astype(jnp.bfloat16)
-        for i, out in enumerate(outs):
-            out[:, at] = y[i * rows : (i + 1) * rows]
-        return 0
-
-    lax.fori_loop(0, width // STEP, columns, 0)
-
-
-def experts(blocks, my_expert, matrices):
+    route = jnp.concatenate([block[:, width:] for block in blocks]).astype(jnp.float32)
+    first, second = route[:, 0:1], route[:, 1:2]
+    w_first = route[:, 2:3] + route[:, 3:4] + route[:, 4:5]
+    w_second = route[:, 5:6] + route[:, 6:7] + route[:, 7:8]
+    w = jnp.where(first == mine, w_first, 0.0) + jnp.where(second == mine, w_second, 0.0)
+    lane = lax.broadcasted_iota(jnp.int32, route.shape, 1).astype(jnp.float32)
+    named = (lane == first).astype(jnp.float32) + (lane == second).astype(jnp.float32)
+    loads[...] = jnp.broadcast_to(jnp.sum(named, axis=0, keepdims=True), loads.shape)
+    for c in range(0, width, STEP):
+        y = jnp.dot(held, down[:, c : c + STEP], preferred_element_type=jnp.float32)
+        y = (y * w).astype(jnp.bfloat16)
+        at = 0
+        for block, out in zip(blocks, outs):
+            out[:, c : c + STEP] = y[at : at + block.shape[0]]
+            at += block.shape[0]
+
+
+def experts(blocks, my_expert, matrices, rolled):
     width, hidden = matrices[0].shape
     flops = 6 * sum(block.shape[0] for block in blocks) * width * hidden
     vmem = pl.BlockSpec(memory_space=pltpu.VMEM)
     blocks = [pltpu.with_memory_space_constraint(block, pltpu.VMEM) for block in blocks]
     *outs, loads = pl.pallas_call(
-        functools.partial(expert_kernel, len(blocks), width),
+        functools.partial(expert_kernel, len(blocks), width, rolled),
         in_specs=[pl.BlockSpec(memory_space=pltpu.SMEM)] + [vmem] * (len(blocks) + 3),
         out_specs=[vmem] * (len(blocks) + 1),
         out_shape=[jax.ShapeDtypeStruct((block.shape[0], width), jnp.bfloat16) for block in blocks]
         + [jax.ShapeDtypeStruct((8, LANES), jnp.float32)],
-        scratch_shapes=[
-            pltpu.VMEM((sum(block.shape[0] for block in blocks), hidden), jnp.bfloat16),
-            pltpu.VMEM((sum(block.shape[0] for block in blocks), LANES), jnp.float32),
-        ],
+        scratch_shapes=[pltpu.VMEM((sum(block.shape[0] for block in blocks), hidden), jnp.bfloat16)],
         cost_estimate=pl.CostEstimate(flops=flops, bytes_accessed=1 << 24, transcendentals=0),
         compiler_params=pltpu.CompilerParams(vmem_limit_bytes=20 << 20),
         name="experts",
@@ -156,8 +167,8 @@
     loads = []
 
     my_expert = staged(my_expert, matrices)
-    low = jnp.concatenate([packed, hop(packed, 1, -1)])
-    high = jnp.concatenate([hop(packed, 1, 1), hop(packed, 1, 2)])
+    low = jnp.concatenate([packed, hop(packed, 1, 2)])
+    high = jnp.concatenate([hop(packed, 1, -1), hop(packed, 1, 1)])
     behind_low = hop(low, 2, 1)
     ahead_high = hop(high, 2, -1)
     ahead_low = hop(low, 2, -1)
@@ -165,18 +176,24 @@
     far_low = hop(behind_low, 2, 1)
     far_high = hop(ahead_high, 2, -1)
 
-    def run(*blocks):
+    def run(name, *blocks):
         shared = [swap(block) for block in blocks]
-        outs, counted = experts((*blocks, *shared), my_expert, matrices)
-        loads.append(counted)
-        mine, others = outs[: len(blocks)], outs[len(blocks) :]
+        if name == "mine":
+            outs, counted = experts((*blocks, *shared), my_expert, matrices, True)
+            loads.append(counted)
+            mine, others = outs[: len(blocks)], outs[len(blocks) :]
+        else:
+            others, counted = experts(shared, my_expert, matrices, name == "first")
+            loads.append(counted)
+            mine, counted = experts(blocks, my_expert, matrices, name == "first")
+            loads.append(counted)
         back = [swap(other) for other in others]
         return lax.optimization_barrier([total_of(*pair) for pair in zip(mine, back)])
 
-    low, high = run(low, high)
-    behind_low, ahead_high = run(behind_low, ahead_high)
-    ahead_low, behind_high = run(ahead_low, behind_high)
-    far_low, far_high = run(far_low, far_high)
+    low, high = run("mine", low, high)
+    behind_low, ahead_high = run("first", behind_low, ahead_high)
+    ahead_low, behind_high = run("second", ahead_low, behind_high)
+    far_low, far_high = run("far", far_low, far_high)
 
     from_ahead_low = hop(behind_low, 2, -1)
     from_behind_high = hop(ahead_high, 2, 1)
@@ -188,17 +205,22 @@
     further = total_of(high, from_ahead_high, from_behind_high, from_far_high)
     plane_sum = total_of(
         near[:rows],
-        hop(near[rows:], 1, 1),
-        hop(further[:rows], 1, -1),
-        hop(further[rows:], 1, 2),
+        hop(near[rows:], 1, 2),
+        hop(further[:rows], 1, 1),
+        hop(further[rows:], 1, -1),
     )
 
     share_rows = rows // n_x
-    shares = plane_sum.reshape(n_x, share_rows, -1)
-    shares = lax.all_to_all(shares, "x", 0, 0, tiled=True)
-    share = jnp.sum(shares.astype(jnp.float32), axis=0).astype(jnp.bfloat16)
-    shares = lax.all_to_all(jnp.broadcast_to(share, shares.shape), "x", 0, 0, tiled=True)
-    half_out = shares.reshape(rows, -1)
+    parts = []
+    for shift in range(n_x):
+        at = (x_at + shift) % n_x
+        part = lax.dynamic_slice_in_dim(plane_sum, at * share_rows, share_rows, 0)
+        parts.append(x_hop(part, shift) if shift else part)
+    share = total_of(*parts)
+    half_out = jnp.zeros(plane_sum.shape, jnp.bfloat16)
+    for shift in range(n_x):
+        part = x_hop(share, shift) if shift else share
+        half_out = lax.dynamic_update_slice_in_dim(half_out, part, ((x_at - shift) % n_x) * share_rows, 0)
     other = swap(half_out)
     mixed = jnp.where(core == 0, jnp.concatenate([half_out, other]), jnp.concatenate([other, half_out]))
     total_loads = sum(loads)[0, :n_experts].astype(jnp.int32)

time: 215 us -> 210 us (0.977)
  blocking collectives: 21.7 us -> 0 us
  waiting for transfers between devices: 91 us -> 102 us
  starting transfers between devices: 42.4 us -> 45.6 us
    all_to_all x2 -> x0, blocking collectives: 21.7 us -> none  [the longest x1 11.2 us: layer(): shares = lax.all_to_all(shares, 'x', 0, 0, tiled=True)]
    ppermute x0 -> x6, starting transfers between devices: none -> 9.7 us  [x_hop(): lax.ppermute(value, 'x', [(i, (i + shift) % size) for i in range(size)])]
    ppermute x18, starting transfers between devices: 38.5 us -> 29.1 us  [hop(): return lax.ppermute(value, PLANE, perm)]
    ppermute x0 -> x6, waiting for transfers between devices: none -> 8.61 us  [x_hop(): lax.ppermute(value, 'x', [(i, (i + shift) % size) for i in range(size)])]
    ppermute x18, waiting for transfers between devices: 84.3 us -> 88.9 us  [hop(): return lax.ppermute(value, PLANE, perm)]
    ppermute x17, starting transfers between devices: 3.84 us -> 6.72 us  [swap(): return lax.ppermute(value, 'c', [(0, 1), (1, 0)])]
    ppermute x17, waiting for transfers between devices: 6.7 us -> 4.25 us  [swap(): return lax.ppermute(value, 'c', [(0, 1), (1, 0)])]
    unnamed x23 -> x19, local copies, waits for them, and re-layouts: 11.6 us -> 10.3 us
  transfers between devices with their start and end apart: 35 -> 41, of which waited for: 12 -> 19; matrix products, arithmetic and copies ran while one was open for 2% -> 4% of each run, Pallas kernels for 18% -> 19%
where the time goes in v1:
time: 210 us; the launch traced here: 207 us
  waiting for transfers between devices  102 us (49%)
  starting transfers between devices  45.6 us (22%)
  Pallas kernels  39.3 us (19%)
  local copies, waits for them, and re-layouts  12.4 us (6%)
  other arithmetic  6.41 us (3%)
    ppermute x18, waiting for transfers between devices, hop(): return lax.ppermute(value, PLANE, perm)  88.9 us
    pallas_call x7, Pallas kernels, experts(): pl.pallas_call(functools.partial(expert_kernel, len(blocks), width, rolle...  38.6 us
    ppermute x18, starting transfers between devices, hop(): return lax.ppermute(value, PLANE, perm)  29.1 us
    unnamed x19, local copies, waits for them, and re-layouts  10.3 us
    ppermute x6, starting transfers between devices, x_hop(): lax.ppermute(value, 'x', [(i, (i + shift) % size) for i in range(size)])  9.7 us
    ppermute x6, waiting for transfers between devices, x_hop(): lax.ppermute(value, 'x', [(i, (i + shift) % size) for i in range(size)])  8.61 us
    ppermute x17, starting transfers between devices, swap(): return lax.ppermute(value, 'c', [(0, 1), (1, 0)])  6.72 us
    ppermute x17, waiting for transfers between devices, swap(): return lax.ppermute(value, 'c', [(0, 1), (1, 0)])  4.25 us
  transfers between devices with their start and end apart: 41, of which 19 were waited for; matrix products, arithmetic and copies ran while one was open for 4% of the time, Pallas kernels for 19%

profile of v1, /device:TPU:2, one launch (start us, length us, event | category | flops | bytes accessed | tf_op | source)
XLA Modules:
  0.0 207.1 jit_solution(11784425843134320592)
XLA Ops:
  4.0 3.3 %collective-permute-start = (bf16[64,4224]{1,0:T(8,128)(2,1)S(1)}, bf16[64,4224]{1,0:T(8,128)(2,1)S(1)}, u32[]{:S(2)}, u32[]{:S(2)}) collective-permute-start(bf16[64,4224]{1,0:T(8,128)(2,1)S(1)} %pack.1), channel_id=1, source_target_pairs={{0,16},{1,65},{8,24},{9,73},{16,0},{17,81},{24,8},{25,89},{32,48},... | collective-permute-start | bytes 1622024 | tf_op jit(solution)/shard_map/ppermute | solution.py:30
  9.3 5.7 %collective-permute-done = bf16[64,4224]{1,0:T(8,128)(2,1)S(1)} collective-permute-done((bf16[64,4224]{1,0:T(8,128)(2,1)S(1)}, bf16[64,4224]{1,0:T(8,128)(2,1)S(1)}, u32[]{:S(2)}, u32[]{:S(2)}) %collective-permute-start) | collective-permute-done | bytes 540704 | tf_op jit(solution)/shard_map/ppermute | solution.py:30
  18.0 3.1 %collective-permute-done.1 = bf16[64,4224]{1,0:T(8,128)(2,1)S(1)} collective-permute-done((bf16[64,4224]{1,0:T(8,128)(2,1)S(1)}, bf16[64,4224]{1,0:T(8,128)(2,1)S(1)}, u32[]{:S(2)}, u32[]{:S(2)}) %collective-permute-start.1) | collective-permute-done | bytes 540704 | tf_op jit(solution)/shard_map/ppermute | solution.py:30
  23.5 4.7 %collective-permute-start.8 = (bf16[128,4224]{1,0:T(8,128)(2,1)}, bf16[128,4224]{1,0:T(8,128)(2,1)}, u32[]{:S(2)}, u32[]{:S(2)}) collective-permute-start(bf16[128,4224]{1,0:T(8,128)(2,1)} %constant_dynamic-update-slice_fusion.refs_1_), channel_id=1, source_target_pairs={{0,96},{1,25},{8,104},{9,1},{16,112},{17,9},{24,120},{25,17},{32,0... | collective-permute-start | bytes 3244040 | tf_op jit(solution)/shard_map/ppermute | solution.py:30
  28.9 4.6 %collective-permute-done.7.refs_0_ = bf16[128,4224]{1,0:T(8,128)(2,1)S(1)} collective-permute-done((bf16[128,4224]{1,0:T(8,128)(2,1)}, bf16[128,4224]{1,0:T(8,128)(2,1)S(1)}, u32[]{:S(2)}, u32[]{:S(2)}) %collective-permute-start.7) | collective-permute-done | bytes 1081376 | tf_op jit(solution)/shard_map/ppermute | solution.py:30
  33.6 7.6 %collective-permute-done.8.refs_1_ = bf16[128,4224]{1,0:T(8,128)(2,1)} collective-permute-done((bf16[128,4224]{1,0:T(8,128)(2,1)}, bf16[128,4224]{1,0:T(8,128)(2,1)}, u32[]{:S(2)}, u32[]{:S(2)}) %collective-permute-start.8) | collective-permute-done | bytes 1081376 | tf_op jit(solution)/shard_map/ppermute | solution.py:30
  41.2 11.6 %collective-permute-done.14.refs_0_ = bf16[128,4224]{1,0:T(8,128)(2,1)S(1)} collective-permute-done((bf16[128,4224]{1,0:T(8,128)(2,1)}, bf16[128,4224]{1,0:T(8,128)(2,1)S(1)}, u32[]{:S(2)}, u32[]{:S(2)}) %collective-permute-start.14) | collective-permute-done | bytes 1081376 | tf_op jit(solution)/shard_map/ppermute | solution.py:30
  60.0 3.7 %collective-permute-start.22 = (bf16[128,4224]{1,0:T(8,128)(2,1)}, bf16[128,4224]{1,0:T(8,128)(2,1)S(1)}, u32[]{:S(2)}, u32[]{:S(2)}) collective-permute-start(bf16[128,4224]{1,0:T(8,128)(2,1)} %collective-permute-done.8.refs_1_), channel_id=1, source_target_pairs={{0,96},{1,25},{8,104},{9,1},{16,112},{17,9},{24,120},{25,17},{32,0... | collective-permute-start | bytes 3244040 | tf_op jit(solution)/shard_map/ppermute | solution.py:30
  64.0 10.0 %experts.7 = (bf16[128,4096]{1,0:T(8,128)(2,1)S(1)}, bf16[128,4096]{1,0:T(8,128)(2,1)S(1)}, bf16[128,4096]{1,0:T(8,128)(2,1)S(1)}, bf16[128,4096]{1,0:T(8,128)(2,1)S(1)}, f32[8,128]{1,0:T(8,128)S(1)}) custom-call(s32[1]{0:T(128)} %stage.1.my_expert, bf16[128,4224]{1,0:T(8,128)(2,1)} %pad_maximum_fusion.refs_0_, ...), custom_call_target="tpu_custom_call" | custom-call | flops 6442450944 | bytes 16777216 | tf_op jit(solution)/shard_map/experts/pallas_call | solution.py:97
  74.7 6.1 %experts.9 = (bf16[128,4096]{1,0:T(8,128)(2,1)S(1)}, bf16[128,4096]{1,0:T(8,128)(2,1)S(1)}, f32[8,128]{1,0:T(8,128)S(1)}) custom-call(s32[1]{0:T(128)} %stage.1.my_expert, bf16[128,4224]{1,0:T(8,128)(2,1)} %collective-permute-done.9.refs_0_, bf16[128,4224]{1,0:T(8,128)(2,1)} %collective-permute-done.10.refs_1_, bf16[4096,512]{1,0:T(8,128)(2,1)S(1)} %bitcast.11, ...), custom_call_target="tpu_custom_call" | custom-call | flops 3221225472 | bytes 16777216 | tf_op jit(solution)/shard_map/experts/pallas_call | solution.py:97
  81.5 5.8 %experts.8 = (bf16[128,4096]{1,0:T(8,128)(2,1)S(1)}, bf16[128,4096]{1,0:T(8,128)(2,1)S(1)}, f32[8,128]{1,0:T(8,128)S(1)}) custom-call(s32[1]{0:T(128)} %stage.1.my_expert, bf16[128,4224]{1,0:T(8,128)(2,1)S(1)} %collective-permute-done.7.refs_0_, bf16[128,4224]{1,0:T(8,128)(2,1)} %collective-permute-done.8.refs_1_, bf16[4096,512]{1,0:T(8,128)(2,1)S(1)} %bitcast.12, ...), custom_call_target="tpu_custom_call" | custom-call | flops 3221225472 | bytes 16777216 | tf_op jit(solution)/shard_map/experts/pallas_call | solution.py:97
  87.3 4.2 %experts.10 = (bf16[128,4096]{1,0:T(8,128)(2,1)S(1)}, bf16[128,4096]{1,0:T(8,128)(2,1)S(1)}, f32[8,128]{1,0:T(8,128)S(1)}) custom-call(s32[1]{0:T(128)} %stage.1.my_expert, bf16[128,4224]{1,0:T(8,128)(2,1)S(1)} %collective-permute-done.14.refs_0_, bf16[128,4224]{1,0:T(8,128)(2,1)S(1)} %collective-permute-done.15.refs_1_, bf16[4096,512]{1,0:T(8,128)(2,1)S(1)} %bitcast.13, ...), custom_call_target="tpu_custom_call" | custom-call | flops 3221225472 | bytes 16777216 | tf_op jit(solution)/shard_map/experts/pallas_call | solution.py:97
  92.1 4.2 %experts.12 = (bf16[128,4096]{1,0:T(8,128)(2,1)S(1)}, bf16[128,4096]{1,0:T(8,128)(2,1)S(1)}, f32[8,128]{1,0:T(8,128)S(1)}) custom-call(s32[1]{0:T(128)} %stage.1.my_expert, bf16[128,4224]{1,0:T(8,128)(2,1)S(1)} %collective-permute-done.21.refs_0_, bf16[128,4224]{1,0:T(8,128)(2,1)S(1)} %collective-permute-done.22.refs_1_, bf16[4096,512]{1,0:T(8,128)(2,1)S(1)} %bitcast.14, ...), custom_call_target="tpu_custom_call" | custom-call | flops 3221225472 | bytes 16777216 | tf_op jit(solution)/shard_map/experts/pallas_call | solution.py:97
  96.9 4.2 %experts.11 = (bf16[128,4096]{1,0:T(8,128)(2,1)S(1)}, bf16[128,4096]{1,0:T(8,128)(2,1)S(1)}, f32[8,128]{1,0:T(8,128)S(1)}) custom-call(s32[1]{0:T(128)} %stage.1.my_expert, bf16[128,4224]{1,0:T(8,128)(2,1)S(1)} %collective-permute-done.16.refs_0_, bf16[128,4224]{1,0:T(8,128)(2,1)S(1)} %collective-permute-done.17.refs_1_, bf16[4096,512]{1,0:T(8,128)(2,1)S(1)} %bitcast.15, ...), custom_call_target="tpu_custom_call" | custom-call | flops 3221225472 | bytes 16777216 | tf_op jit(solution)/shard_map/experts/pallas_call | solution.py:97
  103.9 4.2 %experts.13 = (bf16[128,4096]{1,0:T(8,128)(2,1)S(1)}, bf16[128,4096]{1,0:T(8,128)(2,1)S(1)}, f32[8,128]{1,0:T(8,128)S(1)}) custom-call(s32[1]{0:T(128)} %stage.1.my_expert, bf16[128,4224]{1,0:T(8,128)(2,1)S(1)} %collective-permute-done.23.refs_0_, bf16[128,4224]{1,0:T(8,128)(2,1)S(1)} %collective-permute-done.24.refs_1_, bf16[4096,512]{1,0:T(8,128)(2,1)S(1)} %bitcast.16, ...), custom_call_target="tpu_custom_call" | custom-call | flops 3221225472 | bytes 16777216 | tf_op jit(solution)/shard_map/experts/pallas_call | solution.py:97
  108.1 2.4 %collective-permute-start.25 = (bf16[128,4096]{1,0:T(8,128)(2,1)S(1)}, bf16[128,4096]{1,0:T(8,128)(2,1)S(1)}, u32[]{:S(2)}, u32[]{:S(2)}) collective-permute-start(bf16[128,4096]{1,0:T(8,128)(2,1)S(1)} %get-tuple-element.49), channel_id=1, source_target_pairs={{0,1},{1,0},{2,3},{3,2},{4,5},{5,4},{6,7},{7,6},{8,9},{9,8},{10,11... | collective-permute-start | bytes 3145736 | tf_op jit(solution)/shard_map/ppermute | solution.py:34
  112.8 3.6 %collective-permute-start.29 = (bf16[128,4096]{1,0:T(8,128)(2,1)S(1)}, bf16[128,4096]{1,0:T(8,128)(2,1)S(1)}, u32[]{:S(2)}, u32[]{:S(2)}) collective-permute-start(bf16[128,4096]{1,0:T(8,128)(2,1)S(1)} %add_convert_fusion.4), channel_id=1, source_target_pairs={{0,96},{1,25},{8,104},{9,1},{16,112},{17,9},{24,120},{25,17},{32,0... | collective-permute-start | bytes 3145736 | tf_op jit(solution)/shard_map/ppermute | solution.py:30
  123.1 17.4 %collective-permute-done.29 = bf16[128,4096]{1,0:T(8,128)(2,1)S(1)} collective-permute-done((bf16[128,4096]{1,0:T(8,128)(2,1)S(1)}, bf16[128,4096]{1,0:T(8,128)(2,1)S(1)}, u32[]{:S(2)}, u32[]{:S(2)}) %collective-permute-start.29) | collective-permute-done | bytes 1048608 | tf_op jit(solution)/shard_map/ppermute | solution.py:30
  144.3 4.4 %collective-permute-done.20 = bf16[128,4096]{1,0:T(8,128)(2,1)S(1)} collective-permute-done((bf16[128,4096]{1,0:T(8,128)(2,1)S(1)}, bf16[128,4096]{1,0:T(8,128)(2,1)S(1)}, u32[]{:S(2)}, u32[]{:S(2)}) %collective-permute-start.20) | collective-permute-done | bytes 1048608 | tf_op jit(solution)/shard_map/ppermute | solution.py:30
  148.7 25.0 %collective-permute-done.13 = bf16[128,4096]{1,0:T(8,128)(2,1)S(1)} collective-permute-done((bf16[128,4096]{1,0:T(8,128)(2,1)S(1)}, bf16[128,4096]{1,0:T(8,128)(2,1)S(1)}, u32[]{:S(2)}, u32[]{:S(2)}) %collective-permute-start.13) | collective-permute-done | bytes 1048608 | tf_op jit(solution)/shard_map/ppermute | solution.py:30
  176.2 8.9 %collective-permute-done.28 = bf16[64,4096]{1,0:T(8,128)(2,1)S(1)} collective-permute-done((bf16[64,4096]{1,0:T(8,128)(2,1)S(1)}, bf16[64,4096]{1,0:T(8,128)(2,1)S(1)}, u32[]{:S(2)}, u32[]{:S(2)}) %collective-permute-start.28) | collective-permute-done | bytes 524320 | tf_op jit(solution)/shard_map/ppermute | solution.py:30
  186.0 2.4 %collective-permute-start.35 = (bf16[16,4096]{1,0:T(8,128)(2,1)S(1)}, bf16[16,4096]{1,0:T(8,128)(2,1)S(1)}, u32[]{:S(2)}, u32[]{:S(2)}) collective-permute-start(bf16[16,4096]{1,0:T(8,128)(2,1)S(1)} %get-tuple-element.70), channel_id=1, source_target_pairs={{0,4},{2,6},{4,0},{6,2},{1,5},{3,7},{5,1},{7,3},{8,12},{10,14},{12... | collective-permute-start | bytes 393224 | tf_op jit(solution)/shard_map/ppermute | solution.py:39
  190.4 2.3 %collective-permute-done.35 = bf16[16,4096]{1,0:T(8,128)(2,1)S(1)} collective-permute-done((bf16[16,4096]{1,0:T(8,128)(2,1)S(1)}, bf16[16,4096]{1,0:T(8,128)(2,1)S(1)}, u32[]{:S(2)}, u32[]{:S(2)}) %collective-permute-start.35) | collective-permute-done | bytes 131104 | tf_op jit(solution)/shard_map/ppermute | solution.py:39
  195.6 3.3 %collective-permute-start.38 = (bf16[16,4096]{1,0:T(8,128)(2,1)S(1)}, bf16[16,4096]{1,0:T(8,128)(2,1)S(1)}, u32[]{:S(2)}, u32[]{:S(2)}) collective-permute-start(bf16[16,4096]{1,0:T(8,128)(2,1)S(1)} %get-tuple-element.65), channel_id=1, source_target_pairs={{0,4},{2,6},{4,0},{6,2},{1,5},{3,7},{5,1},{7,3},{8,12},{10,14},{12... | collective-permute-start | bytes 393224 | tf_op jit(solution)/shard_map/ppermute | solution.py:39
  (110 shorter events, 52.9 us)
Async XLA Ops:
  8.3 14.3 %collective-permute-start.2 = (bf16[64,4224]{1,0:T(8,128)(2,1)S(1)}, bf16[64,4224]{1,0:T(8,128)(2,1)S(1)}, u32[]{:S(2)}, u32[]{:S(2)}) collective-permute-start(bf16[64,4224]{1,0:T(8,128)(2,1)S(1)} %pack.1), channel_id=1, source_target_pairs={{0,8},{1,33},{8,16},{9,41},{16,24},{17,49},{24,0},{25,57},{32,40},... | collective-permute-start | bytes 1622024 | tf_op jit(solution)/shard_map/ppermute | solution.py:30
  16.1 17.4 %collective-permute-start.7 = (bf16[128,4224]{1,0:T(8,128)(2,1)}, bf16[128,4224]{1,0:T(8,128)(2,1)S(1)}, u32[]{:S(2)}, u32[]{:S(2)}) collective-permute-start(bf16[128,4224]{1,0:T(8,128)(2,1)} %pad_maximum_fusion.refs_0_), channel_id=1, source_target_pairs={{0,32},{1,9},{8,40},{9,17},{16,48},{17,25},{24,56},{25,1},{32,64},... | collective-permute-start | bytes 3244040 | tf_op jit(solution)/shard_map/ppermute | solution.py:30
  23.5 17.7 %collective-permute-start.8 = (bf16[128,4224]{1,0:T(8,128)(2,1)}, bf16[128,4224]{1,0:T(8,128)(2,1)}, u32[]{:S(2)}, u32[]{:S(2)}) collective-permute-start(bf16[128,4224]{1,0:T(8,128)(2,1)} %constant_dynamic-update-slice_fusion.refs_1_), channel_id=1, source_target_pairs={{0,96},{1,25},{8,104},{9,1},{16,112},{17,9},{24,120},{25,17},{32,0... | collective-permute-start | bytes 3244040 | tf_op jit(solution)/shard_map/ppermute | solution.py:30
  28.2 24.6 %collective-permute-start.14 = (bf16[128,4224]{1,0:T(8,128)(2,1)}, bf16[128,4224]{1,0:T(8,128)(2,1)S(1)}, u32[]{:S(2)}, u32[]{:S(2)}) collective-permute-start(bf16[128,4224]{1,0:T(8,128)(2,1)} %pad_maximum_fusion.refs_0_), channel_id=1, source_target_pairs={{0,96},{1,25},{8,104},{9,1},{16,112},{17,9},{24,120},{25,17},{32,0... | collective-permute-start | bytes 3244040 | tf_op jit(solution)/shard_map/ppermute | solution.py:30
  28.3 31.5 %collective-permute-start.3 = (bf16[128,4224]{1,0:T(8,128)(2,1)}, bf16[128,4224]{1,0:T(8,128)(2,1)}, u32[]{:S(2)}, u32[]{:S(2)}) collective-permute-start(bf16[128,4224]{1,0:T(8,128)(2,1)} %pad_maximum_fusion.refs_0_), channel_id=1, source_target_pairs={{0,1},{1,0},{2,3},{3,2},{4,5},{5,4},{6,7},{7,6},{8,9},{9,8},{10,11... | collective-permute-start | bytes 3244040 | tf_op jit(solution)/shard_map/ppermute | solution.py:34
  28.3 31.6 %collective-permute-start.4 = (bf16[128,4224]{1,0:T(8,128)(2,1)}, bf16[128,4224]{1,0:T(8,128)(2,1)}, u32[]{:S(2)}, u32[]{:S(2)}) collective-permute-start(bf16[128,4224]{1,0:T(8,128)(2,1)} %constant_dynamic-update-slice_fusion.refs_1_), channel_id=1, source_target_pairs={{0,1},{1,0},{2,3},{3,2},{4,5},{5,4},{6,7},{7,6},{8,9},{9,8},{10,11... | collective-permute-start | bytes 3244040 | tf_op jit(solution)/shard_map/ppermute | solution.py:34
  33.5 40.6 %collective-permute-start.15 = (bf16[128,4224]{1,0:T(8,128)(2,1)}, bf16[128,4224]{1,0:T(8,128)(2,1)S(1)}, u32[]{:S(2)}, u32[]{:S(2)}) collective-permute-start(bf16[128,4224]{1,0:T(8,128)(2,1)} %constant_dynamic-update-slice_fusion.refs_1_), channel_id=1, source_target_pairs={{0,32},{1,9},{8,40},{9,17},{16,48},{17,25},{24,56},{25,1},{32,64},... | collective-permute-start | bytes 3244040 | tf_op jit(solution)/shard_map/ppermute | solution.py:30
  41.2 33.4 %collective-permute-start.9 = (bf16[128,4224]{1,0:T(8,128)(2,1)S(1)}, bf16[128,4224]{1,0:T(8,128)(2,1)}, u32[]{:S(2)}, u32[]{:S(2)}) collective-permute-start(bf16[128,4224]{1,0:T(8,128)(2,1)S(1)} %collective-permute-done.7.refs_0_), channel_id=1, source_target_pairs={{0,1},{1,0},{2,3},{3,2},{4,5},{5,4},{6,7},{7,6},{8,9},{9,8},{10,11... | collective-permute-start | bytes 3244040 | tf_op jit(solution)/shard_map/ppermute | solution.py:34
  52.8 22.0 %collective-permute-start.10 = (bf16[128,4224]{1,0:T(8,128)(2,1)}, bf16[128,4224]{1,0:T(8,128)(2,1)}, u32[]{:S(2)}, u32[]{:S(2)}) collective-permute-start(bf16[128,4224]{1,0:T(8,128)(2,1)} %collective-permute-done.8.refs_1_), channel_id=1, source_target_pairs={{0,1},{1,0},{2,3},{3,2},{4,5},{5,4},{6,7},{7,6},{8,9},{9,8},{10,11... | collective-permute-start | bytes 3244040 | tf_op jit(solution)/shard_map/ppermute | solution.py:34
  59.9 31.6 %collective-permute-start.21 = (bf16[128,4224]{1,0:T(8,128)(2,1)S(1)}, bf16[128,4224]{1,0:T(8,128)(2,1)S(1)}, u32[]{:S(2)}, u32[]{:S(2)}) collective-permute-start(bf16[128,4224]{1,0:T(8,128)(2,1)S(1)} %collective-permute-done.7.refs_0_), channel_id=1, source_target_pairs={{0,32},{1,9},{8,40},{9,17},{16,48},{17,25},{24,56},{25,1},{32,64},... | collective-permute-start | bytes 3244040 | tf_op jit(solution)/shard_map/ppermute | solution.py:30
  60.0 31.7 %collective-permute-start.22 = (bf16[128,4224]{1,0:T(8,128)(2,1)}, bf16[128,4224]{1,0:T(8,128)(2,1)S(1)}, u32[]{:S(2)}, u32[]{:S(2)}) collective-permute-start(bf16[128,4224]{1,0:T(8,128)(2,1)} %collective-permute-done.8.refs_1_), channel_id=1, source_target_pairs={{0,96},{1,25},{8,104},{9,1},{16,112},{17,9},{24,120},{25,17},{32,0... | collective-permute-start | bytes 3244040 | tf_op jit(solution)/shard_map/ppermute | solution.py:30
  74.0 22.2 %collective-permute-start.16 = (bf16[128,4224]{1,0:T(8,128)(2,1)S(1)}, bf16[128,4224]{1,0:T(8,128)(2,1)S(1)}, u32[]{:S(2)}, u32[]{:S(2)}) collective-permute-start(bf16[128,4224]{1,0:T(8,128)(2,1)S(1)} %collective-permute-done.14.refs_0_), channel_id=1, source_target_pairs={{0,1},{1,0},{2,3},{3,2},{4,5},{5,4},{6,7},{7,6},{8,9},{9,8},{10,11... | collective-permute-start | bytes 3244040 | tf_op jit(solution)/shard_map/ppermute | solution.py:34
  74.6 21.9 %collective-permute-start.17 = (bf16[128,4224]{1,0:T(8,128)(2,1)S(1)}, bf16[128,4224]{1,0:T(8,128)(2,1)S(1)}, u32[]{:S(2)}, u32[]{:S(2)}) collective-permute-start(bf16[128,4224]{1,0:T(8,128)(2,1)S(1)} %collective-permute-done.15.refs_1_), channel_id=1, source_target_pairs={{0,1},{1,0},{2,3},{3,2},{4,5},{5,4},{6,7},{7,6},{8,9},{9,8},{10,11... | collective-permute-start | bytes 3244040 | tf_op jit(solution)/shard_map/ppermute | solution.py:34
  80.8 20.3 %collective-permute-start.11 = (bf16[128,4096]{1,0:T(8,128)(2,1)S(1)}, bf16[128,4096]{1,0:T(8,128)(2,1)S(1)}, u32[]{:S(2)}, u32[]{:S(2)}) collective-permute-start(bf16[128,4096]{1,0:T(8,128)(2,1)S(1)} %get-tuple-element.39), channel_id=1, source_target_pairs={{0,1},{1,0},{2,3},{3,2},{4,5},{5,4},{6,7},{7,6},{8,9},{9,8},{10,11... | collective-permute-start | bytes 3145736 | tf_op jit(solution)/shard_map/ppermute | solution.py:34
  91.5 26.2 %collective-permute-start.5 = (bf16[128,4096]{1,0:T(8,128)(2,1)S(1)}, bf16[128,4096]{1,0:T(8,128)(2,1)S(1)}, u32[]{:S(2)}, u32[]{:S(2)}) collective-permute-start(bf16[128,4096]{1,0:T(8,128)(2,1)S(1)} %get-tuple-element.34), channel_id=1, source_target_pairs={{0,1},{1,0},{2,3},{3,2},{4,5},{5,4},{6,7},{7,6},{8,9},{9,8},{10,11... | collective-permute-start | bytes 3145736 | tf_op jit(solution)/shard_map/ppermute | solution.py:34
  91.7 26.3 %collective-permute-start.6 = (bf16[128,4096]{1,0:T(8,128)(2,1)S(1)}, bf16[128,4096]{1,0:T(8,128)(2,1)S(1)}, u32[]{:S(2)}, u32[]{:S(2)}) collective-permute-start(bf16[128,4096]{1,0:T(8,128)(2,1)S(1)} %get-tuple-element.36), channel_id=1, source_target_pairs={{0,1},{1,0},{2,3},{3,2},{4,5},{5,4},{6,7},{7,6},{8,9},{9,8},{10,11... | collective-permute-start | bytes 3145736 | tf_op jit(solution)/shard_map/ppermute | solution.py:34
  103.9 17.7 %collective-permute-start.30 = (bf16[128,4096]{1,0:T(8,128)(2,1)S(1)}, bf16[128,4096]{1,0:T(8,128)(2,1)S(1)}, u32[]{:S(2)}, u32[]{:S(2)}) collective-permute-start(bf16[128,4096]{1,0:T(8,128)(2,1)S(1)} %add_convert_fusion.6), channel_id=1, source_target_pairs={{0,32},{1,9},{8,40},{9,17},{16,48},{17,25},{24,56},{25,1},{32,64},... | collective-permute-start | bytes 3145736 | tf_op jit(solution)/shard_map/ppermute | solution.py:30
  112.8 27.7 %collective-permute-start.29 = (bf16[128,4096]{1,0:T(8,128)(2,1)S(1)}, bf16[128,4096]{1,0:T(8,128)(2,1)S(1)}, u32[]{:S(2)}, u32[]{:S(2)}) collective-permute-start(bf16[128,4096]{1,0:T(8,128)(2,1)S(1)} %add_convert_fusion.4), channel_id=1, source_target_pairs={{0,96},{1,25},{8,104},{9,1},{16,112},{17,9},{24,120},{25,17},{32,0... | collective-permute-start | bytes 3145736 | tf_op jit(solution)/shard_map/ppermute | solution.py:30
  116.9 23.6 %collective-permute-start.31 = (bf16[128,4096]{1,0:T(8,128)(2,1)S(1)}, bf16[128,4096]{1,0:T(8,128)(2,1)S(1)}, u32[]{:S(2)}, u32[]{:S(2)}) collective-permute-start(bf16[128,4096]{1,0:T(8,128)(2,1)S(1)} %add_convert_fusion.2), channel_id=1, source_target_pairs={{0,64},{1,17},{8,72},{9,25},{16,80},{17,1},{24,88},{25,9},{32,96},... | collective-permute-start | bytes 3145736 | tf_op jit(solution)/shard_map/ppermute | solution.py:30
  118.2 30.5 %collective-permute-start.20 = (bf16[128,4096]{1,0:T(8,128)(2,1)S(1)}, bf16[128,4096]{1,0:T(8,128)(2,1)S(1)}, u32[]{:S(2)}, u32[]{:S(2)}) collective-permute-start(bf16[128,4096]{1,0:T(8,128)(2,1)S(1)} %add_convert_fusion.5), channel_id=1, source_target_pairs={{0,32},{1,9},{8,40},{9,17},{16,48},{17,25},{24,56},{25,1},{32,64},... | collective-permute-start | bytes 3145736 | tf_op jit(solution)/shard_map/ppermute | solution.py:30
  119.7 54.0 %collective-permute-start.13 = (bf16[128,4096]{1,0:T(8,128)(2,1)S(1)}, bf16[128,4096]{1,0:T(8,128)(2,1)S(1)}, u32[]{:S(2)}, u32[]{:S(2)}) collective-permute-start(bf16[128,4096]{1,0:T(8,128)(2,1)S(1)} %add_convert_fusion.7), channel_id=1, source_target_pairs={{0,96},{1,25},{8,104},{9,1},{16,112},{17,9},{24,120},{25,17},{32,0... | collective-permute-start | bytes 3145736 | tf_op jit(solution)/shard_map/ppermute | solution.py:30
  121.5 52.1 %collective-permute-start.27 = (bf16[128,4096]{1,0:T(8,128)(2,1)S(1)}, bf16[128,4096]{1,0:T(8,128)(2,1)S(1)}, u32[]{:S(2)}, u32[]{:S(2)}) collective-permute-start(bf16[128,4096]{1,0:T(8,128)(2,1)S(1)} %add_convert_fusion.3), channel_id=1, source_target_pairs={{0,64},{1,17},{8,72},{9,25},{16,80},{17,1},{24,88},{25,9},{32,96},... | collective-permute-start | bytes 3145736 | tf_op jit(solution)/shard_map/ppermute | solution.py:30
  142.2 34.0 %collective-permute-start.33 = (bf16[64,4096]{1,0:T(8,128)(2,1)}, bf16[64,4096]{1,0:T(8,128)(2,1)S(1)}, u32[]{:S(2)}, u32[]{:S(2)}) collective-permute-start(bf16[64,4096]{1,0:T(8,128)(2,1)} %get-tuple-element.67), channel_id=1, source_target_pairs={{0,24},{1,97},{8,0},{9,105},{16,8},{17,113},{24,16},{25,121},{32,5... | collective-permute-start | bytes 1572872 | tf_op jit(solution)/shard_map/ppermute | solution.py:30
  142.4 33.8 %collective-permute-start.32 = (bf16[64,4096]{1,0:T(8,128)(2,1)}, bf16[64,4096]{1,0:T(8,128)(2,1)S(1)}, u32[]{:S(2)}, u32[]{:S(2)}) collective-permute-start(bf16[64,4096]{1,0:T(8,128)(2,1)} %get-tuple-element.66), channel_id=1, source_target_pairs={{0,8},{1,33},{8,16},{9,41},{16,24},{17,49},{24,0},{25,57},{32,40},... | collective-permute-start | bytes 1572872 | tf_op jit(solution)/shard_map/ppermute | solution.py:30
  (26 other events, 133.9 us)
